TPU v7x, 32 devices: a whole 2x2x4 slice. The times are simulated.
32 devices in a mesh: expert: 4 (over x, core), replica: 8 (over z, y).
Axes of the slice: x: 2, y: 2, z: 4, core: 2. Of those that a mesh axis runs over, the one named last changes fastest.
Arguments:
- tokens: bfloat16 [8, 1024, 2048], P('replica', 'expert'), may hold values from -6 to 6
- out_grad: bfloat16 [8, 1024, 2048], P('replica', 'expert'), may hold values from -6 to 6
- routes: int32 [8, 1024, 2], P('replica', 'expert'), may hold values from 0 to 3, all different within a row; in each aligned block of 256 rows (0 to 255, 256 to 511, ..., all dimensions but the last counted through in order) at most 256 rows name the same one
- route_weight: bfloat16 [8, 1024, 2], P('replica', 'expert'), may hold values from 0.19921875 to 1
- gate_up_matrix: bfloat16 [8, 4, 2048, 512], P('replica', 'expert'), may hold values from -6 to 6
- down_matrix: bfloat16 [8, 4, 2048, 256], P('replica', 'expert'), may hold values from -6 to 6
- gate_up_velocity: bfloat16 [8, 4, 2048, 512], P('replica', 'expert'), may hold values from -6 to 6
- down_velocity: bfloat16 [8, 4, 2048, 256], P('replica', 'expert'), may hold values from -6 to 6
- partner: int32 [8], replicated, may hold values from 0 to 7, as said below
Outputs:
- token_grad: bfloat16 [8, 1024, 2048], P('replica', 'expert')
- mixed_gate_up: bfloat16 [8, 4, 2048, 512], P('replica', 'expert')
- mixed_down: bfloat16 [8, 4, 2048, 256], P('replica', 'expert')
Inputs may be any that keep to these rules, and one draw needn't show every extreme that they name: `routes`: the rows of one device route at most 256 pairs to any one expert; no row names an expert twice. partner[r] = r xor s for one power of two s below 8, the same s for all r, so replicas are matched in pairs.
All inputs are finite; a program needn't handle non-finite values.
Results may differ from a plain program's by a relative error of at most 0.0065.
Values may be sent and summed in bfloat16 or wider, within the bound.
No kernel may reach another device: no remote copies, remote signals or barrier semaphores. Data moves between devices by JAX's collectives and lax.ppermute only.
A program may use at most 128 MiB of HBM per device.

v0:
```python
import math

import jax
import jax.numpy as jnp
from jax import lax
from jax.sharding import PartitionSpec as P

step_size = 0.2
momentum_decay = 0.9


def shortened(value):

    def short(part):
        return part.astype(jnp.bfloat16) if part.dtype == jnp.float32 else part

    return jax.tree.map(short, value)


def partner_2(block, axis, bit):
    count = lax.axis_size(axis)
    route = []
    for low in range(count):
        high = low | 1 << bit
        if high != low and high < count:
            route += [(low, high), (high, low)]
    return lax.ppermute(block, axis, route)


def contract_leading(left, right):
    return lax.dot_general(
        left, right, (((0,), (0,)), ((), ())), preferred_element_type=jnp.float32
    )


def swap_level(value, level):
    return jax.tree.map(
        lambda part, own: part.astype(own.dtype),
        partner_2(shortened(value), "replica", level),
        value,
    )


def per_device(
    tokens,
    out_grad,
    routes,
    route_weight,
    gate_up_matrix,
    down_matrix,
    gate_up_velocity,
    down_velocity,
    partner,
):
    expert_count = lax.axis_size("expert")
    tok_rows = tokens.shape[1]
    top_count = routes.shape[2]
    feature_width = tokens.shape[2]
    hidden_width = down_matrix.shape[3]
    capacity = 2 * tok_rows * top_count // expert_count
    slot_total = expert_count * capacity
    inv_width = 1.0 / math.sqrt(feature_width)
    inverse_hidden = 1.0 / math.sqrt(hidden_width)
    flat_ids = routes[0].reshape(-1)
    onehot = (flat_ids[:, None] == jnp.arange(expert_count, dtype=jnp.int32)[None, :]).astype(
        jnp.int32
    )
    ranks = jnp.sum((jnp.cumsum(onehot, axis=0) - onehot) * onehot, axis=1)
    slot_lookup = flat_ids * capacity + ranks
    chosen = (slot_lookup[None, :] == jnp.arange(slot_total, dtype=jnp.int32)[:, None]).reshape(
        slot_total, tok_rows, top_count
    )
    picker = jnp.any(chosen, axis=2).astype(jnp.bfloat16)
    weighted = jnp.sum(
        jnp.where(chosen, route_weight[0][None, :, :], jnp.zeros((), jnp.bfloat16)), axis=2
    )
    sent_inputs = jnp.dot(picker, tokens[0], preferred_element_type=jnp.float32).astype(
        jnp.bfloat16
    )
    sent_grads = jnp.dot(weighted, out_grad[0], preferred_element_type=jnp.float32).astype(
        jnp.bfloat16
    )
    recv_inputs, received_gradients = (
        lax.all_to_all(
            sent_inputs.reshape(expert_count, capacity, feature_width),
            "expert",
            split_axis=0,
            concat_axis=0,
            tiled=True,
        ),
        lax.all_to_all(
            sent_grads.reshape(expert_count, capacity, feature_width),
            "expert",
            split_axis=0,
            concat_axis=0,
            tiled=True,
        ),
    )
    input_buffer = recv_inputs.reshape(slot_total, feature_width)
    gradient_buffer = received_gradients.reshape(slot_total, feature_width)
    weight_gu = gate_up_matrix[0, 0]
    down_projection_weight = down_matrix[0, 0]
    pre = jnp.dot(input_buffer, weight_gu, preferred_element_type=jnp.float32) * inv_width
    gate = pre[:, :hidden_width]
    upper = pre[:, hidden_width:]
    active = jax.nn.silu(gate)
    hidden_state = (active * upper).astype(jnp.bfloat16)
    hidden_gradient = (
        jnp.dot(gradient_buffer, down_projection_weight, preferred_element_type=jnp.float32)
        * inverse_hidden
    )
    sigmoid_gate = jax.nn.sigmoid(gate)
    slope = sigmoid_gate * (1.0 + gate * (1.0 - sigmoid_gate))
    pre_grad = jnp.concatenate(
        [hidden_gradient * upper * slope, hidden_gradient * active], axis=1
    ).astype(jnp.bfloat16)
    down_gradient = contract_leading(gradient_buffer, hidden_state) * inverse_hidden
    gate_up_grad = contract_leading(input_buffer, pre_grad) * inv_width
    new_gu = (
        weight_gu.astype(jnp.float32)
        - step_size * (momentum_decay * gate_up_velocity[0, 0].astype(jnp.float32) + gate_up_grad)
    ).astype(jnp.bfloat16)
    next_down_matrix = (
        down_projection_weight.astype(jnp.float32)
        - step_size * (momentum_decay * down_velocity[0, 0].astype(jnp.float32) + down_gradient)
    ).astype(jnp.bfloat16)
    new_gu, next_down_matrix = (new_gu, next_down_matrix)
    replica_count = lax.axis_size("replica")
    bit_total = replica_count.bit_length() - 1
    offset = jnp.bitwise_xor(partner[0], 0)
    level_index = jnp.zeros((), jnp.int32)
    for bit_index in range(bit_total):
        level_index = level_index + bit_index * jnp.bitwise_and(
            jnp.right_shift(offset, bit_index), 1
        )
    joined = jnp.concatenate([new_gu, next_down_matrix], axis=1)
    branches = [functools_partial_level(level) for level in range(bit_total)]
    moved = lax.switch(level_index, branches, joined)
    mixed = (0.5 * (joined.astype(jnp.float32) + moved.astype(jnp.float32))).astype(jnp.bfloat16)
    mixed_gu = mixed[:, : 2 * hidden_width]
    mixed_dn = mixed[:, 2 * hidden_width :]
    paired_gradient = (
        lax.dot_general(
            pre_grad, weight_gu, (((1,), (1,)), ((), ())), preferred_element_type=jnp.float32
        )
        * inv_width
    ).astype(jnp.bfloat16)
    returned = lax.all_to_all(
        paired_gradient.reshape(expert_count, capacity, feature_width),
        "expert",
        split_axis=0,
        concat_axis=0,
        tiled=True,
    )
    combined = contract_leading(picker, returned.reshape(slot_total, feature_width))
    token_grad = combined.astype(jnp.bfloat16)[None]
    return (token_grad, mixed_gu[None, None], mixed_dn[None, None])


def functools_partial_level(level):

    def apply_swap(value):
        return swap_level(value, level)

    return apply_swap


def solution(mesh):
    placed = (
        P("replica", "expert", None),
        P("replica", "expert", None),
        P("replica", "expert", None),
        P("replica", "expert", None),
        P("replica", "expert", None, None),
        P("replica", "expert", None, None),
        P("replica", "expert", None, None),
        P("replica", "expert", None, None),
        P(),
    )
    return jax.shard_map(
        per_device,
        mesh=mesh,
        in_specs=placed,
        out_specs=(
            P("replica", "expert", None),
            P("replica", "expert", None, None),
            P("replica", "expert", None, None),
        ),
        check_vma=False,
    )
```

profile of v0, /device:TPU:0, one launch (start us, length us, event | category | flops | bytes accessed | tf_op | source)
XLA Modules:
  0.0 235.9 jit_solution(4828434784131091851)
XLA Ops:
  0.6 0.0 copy-start
  0.6 0.9 copy.38
  1.6 0.1 eq.43
  1.7 0.1 eq.39
  1.9 1.2 reduce-window.6
  3.1 0.2 slice_reduce_fusion
  3.3 0.2 reduce-window.9
  3.5 0.1 add_bitcast_fusion
  3.6 0.1 reduce_sum.24
  3.8 0.1 copy.41
  3.8 0.4 fusion.12
  4.2 0.0 copy-done
  4.2 3.2 %convolution_convert_fusion = bf16[1024,2048]{1,0:T(8,128)(2,1)} fusion(pred[1024,256]{1,0:T(8,128)(4,1)S(1)} %fusion.12, bf16[1,256,2048]{2,1,0:T(8,128)(2,1)S(1)} %copy-done), kind=kOutput, calls=%fused_computation.6 | convolution fusion | flops 1075838976 | bytes 5505024 | tf_op jit(solution)/shard_map/dot_general | solution.py:77
  7.5 5.1 %all-to-all-start.1 = ((bf16[4,256,2048]{2,1,0:T(8,128)(2,1)}), bf16[4,256,2048]{2,1,0:T(8,128)(2,1)}, u32[]{:S(2)}, u32[]{:S(2)}) async-start(bf16[4,256,2048]{2,1,0:T(8,128)(2,1)} %bitcast.78), calls=%async_computation.1 | async-start | bytes 8388608 | tf_op jit(solution)/shard_map/all_to_all | solution.py:84
  12.5 0.0 copy-done.12
  12.5 0.5 fusion.16
  13.0 0.0 copy-done.11
  13.0 3.2 %convolution_convert_fusion.1 = bf16[1024,2048]{1,0:T(8,128)(2,1)} fusion(bf16[1024,256]{1,0:T(8,128)(2,1)S(1)} %fusion.16, bf16[1,256,2048]{2,1,0:T(8,128)(2,1)S(1)} %copy-done.11), kind=kOutput, calls=%fused_computation.7 | convolution fusion | flops 1075838976 | bytes 5767168 | tf_op jit(solution)/shard_map/dot_general | solution.py:80
  16.2 45.1 %all-to-all-done.1 = bf16[4,256,2048]{2,1,0:T(8,128)(2,1)} async-done(((bf16[4,256,2048]{2,1,0:T(8,128)(2,1)}), bf16[4,256,2048]{2,1,0:T(8,128)(2,1)}, u32[]{:S(2)}, u32[]{:S(2)}) %all-to-all-start.1) | async-done | bytes 4194336 | tf_op jit(solution)/shard_map/all_to_all | solution.py:84
  61.3 4.9 %all-to-all-start = ((bf16[4,256,2048]{2,1,0:T(8,128)(2,1)}), bf16[4,256,2048]{2,1,0:T(8,128)(2,1)}, u32[]{:S(2)}, u32[]{:S(2)}) async-start(bf16[4,256,2048]{2,1,0:T(8,128)(2,1)} %bitcast.77), calls=%async_computation | async-start | bytes 8388608 | tf_op jit(solution)/shard_map/all_to_all | solution.py:91
  66.3 0.0 copy-start.3
  66.3 4.1 %copy.43 = bf16[1,1,2048,512]{2,3,1,0:T(8,128)(2,1)} copy(bf16[1,1,2048,512]{3,2,1,0:T(8,128)(2,1)} %param.16) | data formatting | bytes 4194304 | tf_op args[4]
  70.4 0.0 copy-done.3
  70.4 2.4 %copy.44 = bf16[1,1,2048,512]{2,3,1,0:T(8,128)(2,1)} copy(bf16[1,1,2048,512]{3,2,1,0:T(8,128)(2,1)S(1)} %copy-done.3) | data formatting | bytes 4194304 | tf_op args[6]
  72.8 2.4 %copy.42 = bf16[1,1,2048,256]{2,3,1,0:T(8,128)(2,1)} copy(bf16[1,1,2048,256]{3,2,1,0:T(8,128)(2,1)} %param.17) | data formatting | bytes 2097152 | tf_op args[5]
  75.2 0.0 copy-done.7
  75.2 1.4 copy.45
  76.6 0.0 copy-done.13
  76.7 0.0 copy-done.4
  76.7 0.0 copy-start.8
  76.8 6.0 %fusion.13 = f32[1024,512]{0,1:T(8,128)} fusion(bf16[1024,2048]{1,0:T(8,128)(2,1)} %bitcast.9, bf16[1,1,2048,512]{3,2,1,0:T(8,128)(2,1)S(1)} %copy-done.4), kind=kOutput, calls=%fused_computation.23 | convolution fusion | flops 2148007936 | bytes 8388608 | tf_op jit(solution)/shard_map/dot_general | solution.py:103
  82.7 31.7 %all-to-all-done = bf16[4,256,2048]{2,1,0:T(8,128)(2,1)} async-done(((bf16[4,256,2048]{2,1,0:T(8,128)(2,1)}), bf16[4,256,2048]{2,1,0:T(8,128)(2,1)}, u32[]{:S(2)}, u32[]{:S(2)}) %all-to-all-start) | async-done | bytes 4194336 | tf_op jit(solution)/shard_map/all_to_all | solution.py:91
  114.5 0.0 copy-done.8
  114.5 4.4 %multiply_convert_fusion.4 = (bf16[1024,256]{0,1:T(8,128)(2,1)S(1)}, bf16[1024,256]{0,1:T(8,128)(2,1)S(1)}) fusion(f32[1024,512]{0,1:T(8,128)} %fusion.13, bf16[1024,2048]{1,0:T(8,128)(2,1)} %bitcast.5, bf16[1,1,2048,256]{3,2,1,0:T(8,128)(2,1)S(1)} %copy-done.8), kind=kOutput, calls=%fused_computation.33 | convolution fusion | flops 1077411840 | bytes 8388608 | tf_op jit(solution)/shard_map/dot_general | solution.py:109
  118.9 0.0 copy-start.14
  118.9 0.0 copy-start.16
  118.9 4.4 %multiply_convert_fusion = bf16[1024,2048]{1,0:T(8,128)(2,1)} fusion(bf16[1,1,2048,512]{3,2,1,0:T(8,128)(2,1)S(1)} %copy-done.4, bf16[1024,256]{0,1:T(8,128)(2,1)S(1)} %get-tuple-element.26, bf16[1024,256]{0,1:T(8,128)(2,1)S(1)} %get-tuple-element.25), kind=kOutput, calls=%fused_computation | convolution fusion | flops 2153775104 | bytes 7340032 | tf_op jit(solution)/shard_map/dot_general | solution.py:143
  123.3 0.0 copy-done.14
  123.3 0.0 copy-done.16
  123.3 5.2 %all-to-all-start.2 = ((bf16[4,256,2048]{2,1,0:T(8,128)(2,1)}), bf16[4,256,2048]{2,1,0:T(8,128)(2,1)}, u32[]{:S(2)}, u32[]{:S(2)}) async-start(bf16[4,256,2048]{2,1,0:T(8,128)(2,1)} %bitcast.79), calls=%async_computation.2 | async-start | bytes 8388608 | tf_op jit(solution)/shard_map/all_to_all | solution.py:148
  128.5 0.0 copy-done.9
  128.5 0.0 copy-done.10
  128.5 0.0 copy-start.5
  128.5 0.0 copy-start.6
  128.5 4.5 %fusion.6 = bf16[2048,256]{0,1:T(8,128)(2,1)S(1)} fusion(bf16[1024,2048]{1,0:T(8,128)(2,1)} %bitcast.5, bf16[1,1,2048,256]{2,3,1,0:T(8,128)(2,1)S(1)} %copy-done.10, bf16[1,1,2048,256]{2,3,1,0:T(8,128)(2,1)S(1)} %copy-done.9, f32[1024,512]{0,1:T(8,128)} %fusion.13), kind=kOutput, calls=%fused_computation.14 | convolution fusion | flops 1079508992 | bytes 9437184 | tf_op jit(solution)/shard_map/dot_general | solution.py:31
  133.0 0.0 copy-done.5
  133.0 0.0 copy-done.6
  133.0 0.0 copy-done.15
  133.1 0.0 copy-done.17
  133.1 5.0 %fusion.2 = bf16[2048,512]{0,1:T(8,128)(2,1)S(1)} fusion(bf16[1,1,2048,512]{2,3,1,0:T(8,128)(2,1)S(1)} %copy-done.6, bf16[1024,2048]{1,0:T(8,128)(2,1)} %bitcast.9, bf16[1,1,2048,512]{2,3,1,0:T(8,128)(2,1)S(1)} %copy-done.5, bf16[1024,256]{0,1:T(8,128)(2,1)S(1)} %copy-done.17, bf16[1024,256]{0,1:T(8,128)(2,1)S(1)} %copy-done.15), kind=kOutput, calls=%fused_computation.5 | convolution fusion | flops 2157969408 | bytes 11534336 | tf_op jit(solution)/shard_map/dot_general | solution.py:31
  138.0 2.1 pad_maximum_fusion
  140.1 4.7 %copy.46 = bf16[2048,768]{1,0:T(8,128)(2,1)} copy(bf16[2048,768]{0,1:T(8,128)(2,1)} %pad_maximum_fusion) | data formatting | bytes 6291456 | tf_op jit(solution)/shard_map/concatenate | solution.py:136
  144.8 71.4 %conditional.4 = (bf16[2048,768]{1,0:T(8,128)(2,1)}) conditional(s32[]{:T(128)} %bitcast.16, bf16[2048,768]{1,0:T(8,128)(2,1)} %copy.46, bf16[2048,768]{1,0:T(8,128)(2,1)} %copy.46, bf16[2048,768]{1,0:T(8,128)(2,1)} %copy.46), branch_computations={%region_5.6_spmd, %region_6.7_spmd, %region_7.8_spmd} | conditional | bytes 12582960
  144.8 2.4 %collective-permute-start = (bf16[2048,768]{1,0:T(8,128)(2,1)}, bf16[2048,768]{1,0:T(8,128)(2,1)}, u32[]{:S(2)}, u32[]{:S(2)}) collective-permute-start(bf16[2048,768]{1,0:T(8,128)(2,1)} %param), channel_id=1, source_target_pairs={{0,1},{1,0},{2,3},{3,2},{4,5},{5,4},{6,7},{7,6},{8,9},{9,8},{10,11... | collective-permute-start | bytes 9437192 | tf_op jit(solution)/shard_map/cond/branch_0_fun/ppermute | solution.py:27
  147.2 69.0 %collective-permute-done = bf16[2048,768]{1,0:T(8,128)(2,1)} collective-permute-done((bf16[2048,768]{1,0:T(8,128)(2,1)}, bf16[2048,768]{1,0:T(8,128)(2,1)}, u32[]{:S(2)}, u32[]{:S(2)}) %collective-permute-start) | collective-permute-done | bytes 3145760 | tf_op jit(solution)/shard_map/cond/branch_0_fun/ppermute | solution.py:27
  216.2 4.7 %copy.49 = bf16[2048,768]{0,1:T(8,128)(2,1)} copy(bf16[2048,768]{1,0:T(8,128)(2,1)} %get-tuple-element.27) | data formatting | bytes 6291456 | tf_op jit(solution)/shard_map/conditional.1
  220.9 3.4 %multiply_convert_fusion.1 = bf16[2048,768]{0,1:T(8,128)(2,1)S(1)} fusion(bf16[2048,768]{0,1:T(8,128)(2,1)} %copy.49, bf16[2048,256]{0,1:T(8,128)(2,1)S(1)} %fusion.6, bf16[2048,512]{0,1:T(8,128)(2,1)S(1)} %fusion.2), kind=kLoop, calls=%fused_computation.1 | loop fusion | flops 12582912 | bytes 9437184 | tf_op jit(solution)/shard_map/convert_element_type | solution.py:139
  224.3 1.7 copy-done.2
  226.1 0.1 slice_bitcast_fusion
  226.2 2.5 %copy.50 = bf16[1,1,2048,512]{3,2,1,0:T(8,128)(2,1)} copy(bf16[1,1,2048,512]{2,3,1,0:T(8,128)(2,1)S(1)} %slice_bitcast_fusion) | data formatting | bytes 4194304
  228.7 1.3 slice_bitcast_fusion.1
  230.0 1.3 copy.51
  231.3 0.0 all-to-all-done.2
  231.3 4.5 %fusion.7 = bf16[1,256,2048]{2,1,0:T(8,128)(2,1)} fusion(pred[1024,256]{1,0:T(8,128)(4,1)S(1)} %fusion.12, bf16[1024,2048]{1,0:T(8,128)(2,1)} %bitcast.12), kind=kOutput, calls=%fused_computation.15 | convolution fusion | flops 1074266112 | bytes 5505024 | tf_op jit(solution)/shard_map/dot_general | solution.py:31
  (15 shorter events, 0.1 us)
Async XLA Ops:
  0.6 3.6 %copy-start = (bf16[1,256,2048]{2,1,0:T(8,128)(2,1)S(1)}, bf16[1,256,2048]{2,1,0:T(8,128)(2,1)}, u32[]{:S(2)}) copy-start(bf16[1,256,2048]{2,1,0:T(8,128)(2,1)} %param.12) | copy-start | bytes 3145732
  7.5 5.1 %copy-start.12 = (bf16[1,256,2]{1,2,0:T(2,128)(2,1)S(1)}, bf16[1,256,2]{1,2,0:T(2,128)(2,1)}, u32[]{:S(2)}) copy-start(bf16[1,256,2]{1,2,0:T(2,128)(2,1)} %param.15) | copy-start | bytes 3076
  7.5 5.6 %copy-start.11 = (bf16[1,256,2048]{2,1,0:T(8,128)(2,1)S(1)}, bf16[1,256,2048]{2,1,0:T(8,128)(2,1)}, u32[]{:S(2)}) copy-start(bf16[1,256,2048]{2,1,0:T(8,128)(2,1)} %param.13) | copy-start | bytes 3145732
  7.5 53.9 %all-to-all-start.1 = ((bf16[4,256,2048]{2,1,0:T(8,128)(2,1)}), bf16[4,256,2048]{2,1,0:T(8,128)(2,1)}, u32[]{:S(2)}, u32[]{:S(2)}) async-start(bf16[4,256,2048]{2,1,0:T(8,128)(2,1)} %bitcast.78), calls=%async_computation.1 | async-start | bytes 8388608 | tf_op jit(solution)/shard_map/all_to_all | solution.py:84
  61.3 53.1 %all-to-all-start = ((bf16[4,256,2048]{2,1,0:T(8,128)(2,1)}), bf16[4,256,2048]{2,1,0:T(8,128)(2,1)}, u32[]{:S(2)}, u32[]{:S(2)}) async-start(bf16[4,256,2048]{2,1,0:T(8,128)(2,1)} %bitcast.77), calls=%async_computation | async-start | bytes 8388608 | tf_op jit(solution)/shard_map/all_to_all | solution.py:91
  66.3 4.1 %copy-start.3 = (bf16[1,1,2048,512]{3,2,1,0:T(8,128)(2,1)S(1)}, bf16[1,1,2048,512]{3,2,1,0:T(8,128)(2,1)}, u32[]{:S(2)}) copy-start(bf16[1,1,2048,512]{3,2,1,0:T(8,128)(2,1)} %param.18) | copy-start | bytes 6291460
  70.4 4.9 %copy-start.7 = (bf16[1,1,2048,256]{3,2,1,0:T(8,128)(2,1)S(1)}, bf16[1,1,2048,256]{3,2,1,0:T(8,128)(2,1)}, u32[]{:S(2)}) copy-start(bf16[1,1,2048,256]{3,2,1,0:T(8,128)(2,1)} %param.19) | copy-start | bytes 3145732
  72.8 3.8 %copy-start.13 = (s32[8]{0:T(128)S(1)}, s32[8]{0:T(128)}, u32[]{:S(2)}) copy-start(s32[8]{0:T(128)} %param.20) | copy-start | bytes 100
  72.8 3.9 %copy-start.4 = (bf16[1,1,2048,512]{3,2,1,0:T(8,128)(2,1)S(1)}, bf16[1,1,2048,512]{3,2,1,0:T(8,128)(2,1)}, u32[]{:S(2)}) copy-start(bf16[1,1,2048,512]{3,2,1,0:T(8,128)(2,1)} %param.16) | copy-start | bytes 6291460
  76.7 37.7 %copy-start.8 = (bf16[1,1,2048,256]{3,2,1,0:T(8,128)(2,1)S(1)}, bf16[1,1,2048,256]{3,2,1,0:T(8,128)(2,1)}, u32[]{:S(2)}) copy-start(bf16[1,1,2048,256]{3,2,1,0:T(8,128)(2,1)} %param.17) | copy-start | bytes 3145732
  118.9 4.4 %copy-start.14 = (bf16[1024,256]{0,1:T(8,128)(2,1)}, bf16[1024,256]{0,1:T(8,128)(2,1)S(1)}, u32[]{:S(2)}) copy-start(bf16[1024,256]{0,1:T(8,128)(2,1)S(1)} %get-tuple-element.25) | copy-start | bytes 1572868
  118.9 4.4 %copy-start.16 = (bf16[1024,256]{0,1:T(8,128)(2,1)}, bf16[1024,256]{0,1:T(8,128)(2,1)S(1)}, u32[]{:S(2)}) copy-start(bf16[1024,256]{0,1:T(8,128)(2,1)S(1)} %get-tuple-element.26) | copy-start | bytes 1572868
  123.3 5.2 %copy-start.9 = (bf16[1,1,2048,256]{2,3,1,0:T(8,128)(2,1)S(1)}, bf16[1,1,2048,256]{2,3,1,0:T(8,128)(2,1)}, u32[]{:S(2)}) copy-start(bf16[1,1,2048,256]{2,3,1,0:T(8,128)(2,1)} %copy.42) | copy-start | bytes 3145732
  123.3 5.2 %copy-start.10 = (bf16[1,1,2048,256]{2,3,1,0:T(8,128)(2,1)S(1)}, bf16[1,1,2048,256]{2,3,1,0:T(8,128)(2,1)}, u32[]{:S(2)}) copy-start(bf16[1,1,2048,256]{2,3,1,0:T(8,128)(2,1)} %copy.45) | copy-start | bytes 3145732
  123.3 108.0 %all-to-all-start.2 = ((bf16[4,256,2048]{2,1,0:T(8,128)(2,1)}), bf16[4,256,2048]{2,1,0:T(8,128)(2,1)}, u32[]{:S(2)}, u32[]{:S(2)}) async-start(bf16[4,256,2048]{2,1,0:T(8,128)(2,1)} %bitcast.79), calls=%async_computation.2 | async-start | bytes 8388608 | tf_op jit(solution)/shard_map/all_to_all | solution.py:148
  128.5 4.5 %copy-start.5 = (bf16[1,1,2048,512]{2,3,1,0:T(8,128)(2,1)S(1)}, bf16[1,1,2048,512]{2,3,1,0:T(8,128)(2,1)}, u32[]{:S(2)}) copy-start(bf16[1,1,2048,512]{2,3,1,0:T(8,128)(2,1)} %copy.43) | copy-start | bytes 6291460
  128.5 4.5 %copy-start.6 = (bf16[1,1,2048,512]{2,3,1,0:T(8,128)(2,1)S(1)}, bf16[1,1,2048,512]{2,3,1,0:T(8,128)(2,1)}, u32[]{:S(2)}) copy-start(bf16[1,1,2048,512]{2,3,1,0:T(8,128)(2,1)} %copy.44) | copy-start | bytes 6291460
  128.5 4.5 %copy-start.15 = (bf16[1024,256]{0,1:T(8,128)(2,1)S(1)}, bf16[1024,256]{0,1:T(8,128)(2,1)}, u32[]{:S(2)}) copy-start(bf16[1024,256]{0,1:T(8,128)(2,1)} %copy-done.14) | copy-start | bytes 1572868
  128.5 4.5 %copy-start.17 = (bf16[1024,256]{0,1:T(8,128)(2,1)S(1)}, bf16[1024,256]{0,1:T(8,128)(2,1)}, u32[]{:S(2)}) copy-start(bf16[1024,256]{0,1:T(8,128)(2,1)} %copy-done.16) | copy-start | bytes 1572868
  144.8 71.4 %collective-permute-start = (bf16[2048,768]{1,0:T(8,128)(2,1)}, bf16[2048,768]{1,0:T(8,128)(2,1)}, u32[]{:S(2)}, u32[]{:S(2)}) collective-permute-start(bf16[2048,768]{1,0:T(8,128)(2,1)} %param), channel_id=1, source_target_pairs={{0,1},{1,0},{2,3},{3,2},{4,5},{5,4},{6,7},{7,6},{8,9},{9,8},{10,11... | collective-permute-start | bytes 9437192 | tf_op jit(solution)/shard_map/cond/branch_0_fun/ppermute | solution.py:27
  224.3 1.7 copy-start.2
  231.3 4.5 %copy-start.1 = (bf16[1,256,2048]{2,1,0:T(8,128)(2,1)S(1)}, bf16[1,256,2048]{2,1,0:T(8,128)(2,1)}, u32[]{:S(2)}) copy-start(bf16[1,256,2048]{2,1,0:T(8,128)(2,1)} %param.12) | copy-start | bytes 3145732
where the time goes:
time: 237 us; the launch traced here: 236 us
  waiting for transfers between devices  146 us (62%)
  matrix products  35.2 us (15%)
  local copies, waits for them, and re-layouts  28.5 us (12%)
  starting transfers between devices  17.5 us (7%)
  other arithmetic  7.83 us (3%)
    ppermute x1, waiting for transfers between devices, partner_2(): return lax.ppermute(block, axis, route)  69 us
    all_to_all x1, waiting for transfers between devices, per_device(): lax.all_to_all(sent_inputs.reshape(expert_count, capacity, feature_width)...  45.1 us
    all_to_all x1, waiting for transfers between devices, per_device(): lax.all_to_all(sent_grads.reshape(expert_count, capacity, feature_width),...  31.7 us
    unnamed x43, local copies, waits for them, and re-layouts  16.9 us
    dot_general x3, matrix products, contract_leading(): lax.dot_general(left, right, (((0,), (0,)), ((), ())), preferred_element_...  14 us
    dot_general x1, matrix products, per_device(): jnp.dot(input_buffer, weight_gu, preferred_element_type=jnp.float32)  5.97 us
    all_to_all x1, starting transfers between devices, per_device(): lax.all_to_all(paired_gradient.reshape(expert_count, capacity, feature_wi...  5.16 us
    all_to_all x1, starting transfers between devices, per_device(): lax.all_to_all(sent_inputs.reshape(expert_count, capacity, feature_width)...  5.06 us
  transfers between devices with their start and end apart: 4, of which 3 were waited for; matrix products, arithmetic and copies ran while one was open for 21% of the time, Pallas kernels for 0%

commit v1 on v0

--- a/solution.py
+++ b/solution.py
@@ -1,9 +1,13 @@
+import functools
 import math
 
 import jax
 import jax.numpy as jnp
 from jax import lax
+from jax.experimental import pallas as pl
+from jax.experimental.pallas import tpu as pltpu
 from jax.sharding import PartitionSpec as P
+
 
 step_size = 0.2
 momentum_decay = 0.9
@@ -41,7 +45,7 @@
     )
 
 
-def per_device(
+def routed_layer(
     tokens,
     out_grad,
     routes,
@@ -134,7 +138,7 @@
             jnp.right_shift(offset, bit_index), 1
         )
     joined = jnp.concatenate([new_gu, next_down_matrix], axis=1)
-    branches = [functools_partial_level(level) for level in range(bit_total)]
+    branches = [functools.partial(swap_level, level=level) for level in range(bit_total)]
     moved = lax.switch(level_index, branches, joined)
     mixed = (0.5 * (joined.astype(jnp.float32) + moved.astype(jnp.float32))).astype(jnp.bfloat16)
     mixed_gu = mixed[:, : 2 * hidden_width]
@@ -157,12 +161,291 @@
     return (token_grad, mixed_gu[None, None], mixed_dn[None, None])
 
 
-def functools_partial_level(level):
-
-    def apply_swap(value):
-        return swap_level(value, level)
-
-    return apply_swap
+def swap(block, axis, bit):
+    count = lax.axis_size(axis)
+    return lax.ppermute(block, axis, [(i, i ^ (1 << bit)) for i in range(count)])
+
+
+def call(body, outs, *args, grid=None, in_specs=None, out_specs=None, flops=0, aliases=None):
+    size = sum(a.size * a.dtype.itemsize for a in args)
+    size += sum(math.prod(o.shape) * o.dtype.itemsize for o in outs)
+    options = {}
+    if grid is not None:
+        options = dict(grid=grid, in_specs=in_specs, out_specs=out_specs)
+    return pl.pallas_call(
+        body,
+        out_shape=outs,
+        input_output_aliases=aliases or {},
+        compiler_params=pltpu.CompilerParams(vmem_limit_bytes=40 << 20),
+        cost_estimate=pl.CostEstimate(flops=max(flops, size), bytes_accessed=size, transcendentals=0),
+        **options,
+    )(*args)
+
+
+def shape(dims, dtype=jnp.bfloat16):
+    return jax.ShapeDtypeStruct(dims, dtype)
+
+
+def mm(left, right, dims=(1, 0)):
+    return lax.dot_general(
+        left, right, (((dims[0],), (dims[1],)), ((), ())), preferred_element_type=jnp.float32
+    )
+
+
+def split_body(count, wide, x_ref, *out_refs):
+    for i in range(count):
+        out_refs[i][...] = x_ref[:, i * wide : (i + 1) * wide]
+
+
+def forward_body(scale, hidden, x_ref, w_ref, state_ref, first_ref, second_ref, turned_ref):
+    x = x_ref[...]
+    pre = mm(x, w_ref[...]) * scale
+    gate, up = pre[:, :hidden], pre[:, hidden:]
+    sig = jax.nn.sigmoid(gate)
+    active = gate * sig
+    state_ref[...] = (active * up).astype(jnp.bfloat16)
+    first_ref[...] = up * (sig * (1.0 + gate * (1.0 - sig)))
+    second_ref[...] = active
+    turned_ref[...] = x.T
+
+
+def scaled(me, grad, share):
+    lane = lax.broadcasted_iota(jnp.int32, share.shape, 1)
+    own = jnp.sum(jnp.where(lane == me, share.astype(jnp.float32), 0.0), axis=1, keepdims=True)
+    return (grad.astype(jnp.float32) * own).astype(jnp.bfloat16)
+
+
+def near_grad_body(me_ref, ga_ref, gb_ref, sa_ref, sb_ref, ha_ref, hb_ref, w_ref, d_ref, oa_ref, ob_ref):
+    me = me_ref[0]
+    w = w_ref[...]
+
+    @pl.when(pl.program_id(0) == 0)
+    def _():
+        oa_ref[...] = jnp.zeros_like(oa_ref)
+        ob_ref[...] = jnp.zeros_like(ob_ref)
+
+    ga = scaled(me, ga_ref[...], sa_ref[...])
+    gb = scaled(me, gb_ref[...], sb_ref[...])
+    d_ref[...] = mm(ga, ha_ref[...], (0, 0)) + mm(gb, hb_ref[...], (0, 0))
+    oa_ref[...] += mm(ga, w)
+    ob_ref[...] += mm(gb, w)
+
+
+def moved_weight(weight, speed, grad):
+    value = weight.astype(jnp.float32) - step_size * (momentum_decay * speed.astype(jnp.float32) + grad)
+    return value.astype(jnp.bfloat16)
+
+
+def far_grad_body(
+    scale, me_ref, gc_ref, gd_ref, sc_ref, sd_ref, hc_ref, hd_ref, w_ref, v_ref, d_ref, ic_ref, id_ref,
+    u_ref, oc_ref, od_ref,
+):
+    me = me_ref[0]
+    w = w_ref[...]
+    gc = scaled(me, gc_ref[...], sc_ref[...])
+    gd = scaled(me, gd_ref[...], sd_ref[...])
+    d = d_ref[...] + mm(gc, hc_ref[...], (0, 0)) + mm(gd, hd_ref[...], (0, 0))
+    u_ref[...] = moved_weight(w, v_ref[...], d * scale)
+    oc_ref[...] = ic_ref[...] + mm(gc, w)
+    od_ref[...] = id_ref[...] + mm(gd, w)
+
+
+def pre_grad_of(scale, grad, first, second):
+    grad = grad * scale
+    return jnp.concatenate([(grad * first), (grad * second)], axis=1).astype(jnp.bfloat16)
+
+
+def near_weight_body(scale, ga_ref, gb_ref, fa_ref, fb_ref, sa_ref, sb_ref, ta_ref, tb_ref, d_ref, pa_ref, pb_ref):
+    @pl.when(pl.program_id(0) == 0)
+    def _():
+        pa_ref[...] = pre_grad_of(scale, ga_ref[...], fa_ref[...], sa_ref[...])
+        pb_ref[...] = pre_grad_of(scale, gb_ref[...], fb_ref[...], sb_ref[...])
+
+    d_ref[...] = mm(ta_ref[...], pa_ref[...]) + mm(tb_ref[...], pb_ref[...])
+
+
+def far_pre_grad_body(scale, gc_ref, gd_ref, fc_ref, fd_ref, sc_ref, sd_ref, pc_ref, pd_ref):
+    pc_ref[...] = pre_grad_of(scale, gc_ref[...], fc_ref[...], sc_ref[...])
+    pd_ref[...] = pre_grad_of(scale, gd_ref[...], fd_ref[...], sd_ref[...])
+
+
+def far_weight_body(scale, pc_ref, pd_ref, tc_ref, td_ref, d_ref, w_ref, v_ref, u_ref):
+    d = d_ref[...] + mm(tc_ref[...], pc_ref[...]) + mm(td_ref[...], pd_ref[...])
+    u_ref[...] = moved_weight(w_ref[...], v_ref[...], d * scale)
+
+
+def back_body(scale, p_ref, w_ref, *refs):
+    value = (mm(p_ref[...], w_ref[...], (1, 1)) * scale).astype(jnp.bfloat16)
+    if len(refs) > 1:
+        total = value.astype(jnp.float32)
+        for ref in refs[:-1]:
+            total = total + ref[...].astype(jnp.float32)
+        value = total.astype(jnp.bfloat16)
+    refs[-1][...] = value
+
+
+def mix_body(own_ref, moved_ref, *refs):
+    total = own_ref[...].astype(jnp.float32) + moved_ref[...].astype(jnp.float32)
+    refs[-1][...] = (0.5 * total).astype(jnp.bfloat16)
+
+
+def dense_layer(level, me, tokens, out_grad, shares, gate_up, down, gate_up_velocity, down_velocity):
+    return dense_steps(
+        level, me, tokens, out_grad, shares, gate_up, down, gate_up_velocity, down_velocity
+    )
+
+
+def dense_steps(level, me, tokens, out_grad, shares, gate_up, down, gate_up_velocity, down_velocity):
+    grad_parts, weight_parts = GRAD_PARTS, WEIGHT_PARTS
+    rows, width = tokens.shape
+    hidden = down.shape[1]
+    inv_width = 1.0 / math.sqrt(width)
+    inv_hidden = 1.0 / math.sqrt(hidden)
+    core, chip = 0, 1
+    wide, high = width // grad_parts, width // weight_parts
+    f32 = jnp.float32
+    half = shape((rows, hidden), f32)
+    scalar = pl.BlockSpec(memory_space=pltpu.SMEM)
+
+    def whole(a):
+        return pl.BlockSpec(a.shape, lambda i: (0,) * len(a.shape))
+
+    chip_tokens = swap(tokens, "expert", chip)
+    grads = call(
+        functools.partial(split_body, grad_parts, wide),
+        [shape((rows, wide))] * grad_parts, out_grad,
+    )
+    chip_grads = [swap(grads[i], "expert", chip) for i in range(grad_parts)]
+    core_tokens = swap(tokens, "expert", core)
+    core_shares = swap(shares, "expert", core)
+    chip_shares = swap(shares, "expert", chip)
+    core_grads = swap(out_grad, "expert", core)
+    far_shares = swap(chip_shares, "expert", core)
+    far_tokens = swap(chip_tokens, "expert", core)
+    far_grads = [swap(g, "expert", core) for g in chip_grads]
+
+    def forward(x):
+        return call(
+            functools.partial(forward_body, inv_width, hidden),
+            [shape((rows, hidden)), half, half, shape((width, rows))], x, gate_up,
+            flops=4 * rows * width * hidden,
+        )
+
+    ha, fa, sa, ta = forward(tokens)
+    hb, fb, sb, tb = forward(core_tokens)
+    col = pl.BlockSpec((rows, wide), lambda i: (0, i))
+    row = pl.BlockSpec((wide, hidden), lambda i: (i, 0))
+    near_down, ga, gb = call(
+        near_grad_body, [shape((width, hidden), f32), half, half],
+        me, out_grad, core_grads, shares, core_shares, ha, hb, down,
+        grid=(grad_parts,),
+        in_specs=[scalar, col, col, whole(shares), whole(shares), whole(ha), whole(hb), row],
+        out_specs=[row, whole(half), whole(half)],
+        flops=8 * rows * width * hidden,
+    )
+    tall = pl.BlockSpec((high, rows), lambda i: (i, 0))
+    full = pl.BlockSpec((high, 2 * hidden), lambda i: (i, 0))
+    pair = shape((rows, 2 * hidden))
+    near_gu, pa, pb = call(
+        functools.partial(near_weight_body, inv_hidden),
+        [shape(gate_up.shape, f32), pair, pair], ga, gb, fa, fb, sa, sb, ta, tb,
+        grid=(weight_parts,),
+        in_specs=[whole(half)] * 6 + [tall, tall],
+        out_specs=[full, whole(pair), whole(pair)],
+        flops=8 * rows * width * hidden,
+    )
+    hc, fc, sc, tc = forward(chip_tokens)
+    hd, fd, sd, td = forward(far_tokens)
+    gc = gd = jnp.zeros(half.shape, f32)
+    own_down, moved_down = [], []
+    for i in range(grad_parts):
+        part = pl.BlockSpec((wide, hidden), lambda _, i=i: (i, 0))
+        u, gc, gd = call(
+            functools.partial(far_grad_body, inv_hidden),
+            [shape((wide, hidden)), half, half],
+            me, chip_grads[i], far_grads[i], chip_shares, far_shares, hc, hd,
+            down, down_velocity, near_down, gc, gd,
+            grid=(1,),
+            in_specs=[scalar, whole(grads[i]), whole(grads[i]), whole(shares), whole(shares),
+                      whole(hc), whole(hd), part, part, part, whole(half), whole(half)],
+            out_specs=[whole(shape((wide, hidden))), whole(half), whole(half)],
+            flops=8 * rows * wide * hidden,
+        )
+        own_down.append(u)
+        moved_down.append(swap(u, "replica", level))
+    pc, pd = call(functools.partial(far_pre_grad_body, inv_hidden), [pair, pair], gc, gd, fc, fd, sc, sd)
+    own_gu, moved_gu = [], []
+    for i in range(weight_parts):
+        part = pl.BlockSpec((high, 2 * hidden), lambda _, i=i: (i, 0))
+        turned = pl.BlockSpec((high, rows), lambda _, i=i: (i, 0))
+        u = call(
+            functools.partial(far_weight_body, inv_width),
+            [shape((high, 2 * hidden))], pc, pd, tc, td, near_gu, gate_up, gate_up_velocity,
+            grid=(1,),
+            in_specs=[whole(pair), whole(pair), turned, turned, part, part, part],
+            out_specs=[whole(shape((high, 2 * hidden)))],
+            flops=8 * rows * high * hidden,
+        )[0]
+        own_gu.append(u)
+        moved_gu.append(swap(u, "replica", level))
+
+    def back(p, *more):
+        return call(
+            functools.partial(back_body, inv_width), [shape((rows, width))], p, gate_up, *more,
+            flops=4 * rows * width * hidden,
+        )[0]
+
+    for_far = swap(back(pd), "expert", core)
+    for_core = swap(back(pb), "expert", core)
+    for_chip = swap(back(pc, for_far), "expert", chip)
+    token_grad = back(pa, for_core, for_chip)
+
+    def mixed(own, moved, total):
+        out = None
+        for i, (a, b) in enumerate(zip(own, moved)):
+            spot = pl.BlockSpec(a.shape, lambda _, i=i: (i, 0))
+            args = (a, b) if out is None else (a, b, out)
+            specs = [whole(a), whole(a)] + [pl.BlockSpec(memory_space=pl.ANY)] * (len(args) - 2)
+            out = call(
+                mix_body, [shape(total)], *args,
+                grid=(1,), in_specs=specs, out_specs=[spot],
+                aliases={2: 0} if out is not None else None,
+            )[0]
+        return out
+
+    mixed_dn = mixed(own_down, moved_down, down.shape)
+    mixed_gu = mixed(own_gu, moved_gu, gate_up.shape)
+    return token_grad[None], mixed_gu[None, None], mixed_dn[None, None]
+
+
+GRAD_PARTS, WEIGHT_PARTS = 4, 4
+
+
+def per_device(
+    tokens, out_grad, routes, route_weight, gate_up_matrix, down_matrix, gate_up_velocity, down_velocity, partner
+):
+    experts = lax.axis_size("expert")
+    _, top_count = routes.shape[1:]
+    if not dense(experts, top_count):
+        return routed_layer(
+            tokens, out_grad, routes, route_weight, gate_up_matrix, down_matrix, gate_up_velocity, down_velocity, partner
+        )
+    levels = lax.axis_size("replica").bit_length() - 1
+    level = sum(
+        bit * jnp.bitwise_and(jnp.right_shift(partner[0], bit), 1) for bit in range(levels)
+    )
+    named = routes[0][:, :, None] == jnp.arange(experts, dtype=jnp.int32)
+    shares = jnp.sum(jnp.where(named, route_weight[0][:, :, None], jnp.zeros((), jnp.bfloat16)), axis=1)
+    me = lax.axis_index("expert").reshape(1)
+    branches = [functools.partial(dense_layer, i) for i in range(levels)]
+    return lax.switch(
+        level, branches, me, tokens[0], out_grad[0], shares, gate_up_matrix[0, 0], down_matrix[0, 0],
+        gate_up_velocity[0, 0], down_velocity[0, 0],
+    )
+
+
+def dense(experts, top_count):
+    return experts == 4 and 2 * top_count >= experts
 
 
 def solution(mesh):

time: 237 us -> 164 us (0.69); the launches traced: 236 us -> 160 us
  waiting for transfers between devices: 146 us -> 98.7 us
  matrix products: 35.2 us -> 0 us
  local copies, waits for them, and re-layouts: 28.5 us -> 2.98 us
  Pallas kernels: 0 us -> 22.6 us
  loops' own time: 0.01 us -> 8.8 us
  other arithmetic: 7.83 us -> 0.71 us
  starting transfers between devices: 17.5 us -> 23.5 us
    all_to_all x3 -> x0, waiting for transfers between devices: 76.8 us -> none  [the longest x1 45.1 us: per_device(): lax.all_to_all(sent_inputs.reshape(expert_count, capacity, feature_width)...]
    dot_general x8 -> x0, matrix products: 35.2 us -> none  [the longest x3 14 us: contract_leading(): lax.dot_general(left, right, (((0,), (0,)), ((), ())), preferred_element_...]
    ppermute x1 -> x26, waiting for transfers between devices: 69 us -> 98.7 us  [swap(): return lax.ppermute(block, axis, [(i, i ^ 1 << bit) for i in range(count)])]
    pallas_call x0 -> x28, Pallas kernels: none -> 22.6 us  [call(): pl.pallas_call(body, out_shape=outs, input_output_aliases=aliases or {},...]
    ppermute x1 -> x26, starting transfers between devices: 2.39 us -> 23.5 us  [swap(): return lax.ppermute(block, axis, [(i, i ^ 1 << bit) for i in range(count)])]
    unnamed x43 -> x0, local copies, waits for them, and re-layouts: 16.9 us -> none
    all_to_all x3 -> x0, starting transfers between devices: 15.1 us -> none  [the longest x1 5.16 us: per_device(): lax.all_to_all(paired_gradient.reshape(expert_count, capacity, feature_wi...]
    another operation x0 -> x1, loops' own time: none -> 8.8 us  [per_device(): lax.switch(level, branches, me, tokens[0], out_grad[0], shares, gate_up_m...]
  transfers between devices with their start and end apart: 4 -> 26, of which waited for: 3 -> 13; matrix products, arithmetic and copies ran while one was open for 21% -> 1% of each run, Pallas kernels for 0% -> 12%
where the time goes in v1:
time: 164 us; the launch traced here: 160 us
  waiting for transfers between devices  98.7 us (60%)
  starting transfers between devices  23.5 us (14%)
  Pallas kernels  22.6 us (14%)
  loops' own time  8.8 us (5%)
  between operations  3 us (2%)
  local copies, waits for them, and re-layouts  2.98 us (2%)
    ppermute x26, waiting for transfers between devices, swap(): return lax.ppermute(block, axis, [(i, i ^ 1 << bit) for i in range(count)])  98.7 us
    ppermute x26, starting transfers between devices, swap(): return lax.ppermute(block, axis, [(i, i ^ 1 << bit) for i in range(count)])  23.5 us
    pallas_call x28, Pallas kernels, call(): pl.pallas_call(body, out_shape=outs, input_output_aliases=aliases or {},...  22.6 us
    another operation x1, loops' own time, per_device(): lax.switch(level, branches, me, tokens[0], out_grad[0], shares, gate_up_m...  8.8 us
  transfers between devices with their start and end apart: 26, of which 13 were waited for; matrix products, arithmetic and copies ran while one was open for 1% of the time, Pallas kernels for 12%

profile of v1, /device:TPU:0, one launch (start us, length us, event | category | flops | bytes accessed | tf_op | source)
XLA Modules:
  0.0 160.4 jit_solution(7603610098814957902)
XLA Ops:
  1.9 157.4 %conditional.1 = (bf16[1,256,2048]{2,1,0:T(8,128)(2,1)}, bf16[1,1,2048,512]{3,2,1,0:T(8,128)(2,1)}, bf16[1,1,2048,256]{3,2,1,0:T(8,128)(2,1)}) conditional(s32[]{:T(128)} %bitcast.36, (bf16[1,256,2048]{2,1,0:T(8,128)(2,1)}, s32[1,256,2]{1,2,0:T(2,128)}, bf16[1,256,2048]{2,1,0:T(8,128)(2,1)}, bf16[1,1,2048,512]{3,2,1,0:T(8,128)(2,1)}, ...), branch_computations={%region_1.2_spmd, %region_2.3_spmd, %region_3.4_spmd} | conditional | flops 8622445568 | bytes 250149152 | solution.py:441
  2.0 3.0 %collective-permute-start.8 = (bf16[256,2048]{1,0:T(8,128)(2,1)}, bf16[256,2048]{1,0:T(8,128)(2,1)S(1)}, u32[]{:S(2)}, u32[]{:S(2)}) collective-permute-start(bf16[256,2048]{1,0:T(8,128)(2,1)} %bitcast.119), channel_id=1, source_target_pairs={{0,16},{8,24},{16,0},{24,8},{1,17},{9,25},{17,1},{25,9},{2,18},{10... | collective-permute-start | bytes 3145736 | tf_op jit(solution)/shard_map/cond/branch_0_fun/ppermute | solution.py:166
  5.0 0.5 collective-permute-start.2
  5.5 22.9 %collective-permute-done.8.x_ref = bf16[256,2048]{1,0:T(8,128)(2,1)S(1)} collective-permute-done((bf16[256,2048]{1,0:T(8,128)(2,1)}, bf16[256,2048]{1,0:T(8,128)(2,1)S(1)}, u32[]{:S(2)}, u32[]{:S(2)}) %collective-permute-start.8) | collective-permute-done | bytes 1048608 | tf_op jit(solution)/shard_map/cond/branch_0_fun/ppermute | solution.py:166
  28.4 1.9 %branch_0_fun.33 = (bf16[256,512]{1,0:T(8,128)(2,1)S(1)}, bf16[256,512]{1,0:T(8,128)(2,1)S(1)}, bf16[256,512]{1,0:T(8,128)(2,1)S(1)}, bf16[256,512]{1,0:T(8,128)(2,1)}) custom-call(bf16[256,2048]{1,0:T(8,128)(2,1)} %bitcast.129), custom_call_target="tpu_custom_call" | custom-call | flops 2097152 | bytes 2097152 | tf_op jit(solution)/shard_map/cond/branch_0_fun/pallas_call | solution.py:175
  30.3 0.7 copy-done
  31.0 0.7 copy-done.3
  31.7 0.7 copy-done.6
  32.4 1.7 %collective-permute-start.4 = (bf16[256,512]{1,0:T(8,128)(2,1)}, bf16[256,512]{1,0:T(8,128)(2,1)S(1)}, u32[]{:S(2)}, u32[]{:S(2)}) collective-permute-start(bf16[256,512]{1,0:T(8,128)(2,1)} %get-tuple-element.66), channel_id=1, source_target_pairs={{0,16},{8,24},{16,0},{24,8},{1,17},{9,25},{17,1},{25,9},{2,18},{10... | collective-permute-start | bytes 786440 | tf_op jit(solution)/shard_map/cond/branch_0_fun/ppermute | solution.py:166
  34.2 0.7 fusion
  34.9 0.1 copy.64.sa_ref
  35.0 0.4 collective-permute-start.6
  35.4 7.4 %collective-permute-done.6.sc_ref = bf16[256,4]{1,0:T(8,128)(2,1)S(1)} collective-permute-done((bf16[256,4]{1,0:T(8,128)(2,1)S(1)}, bf16[256,4]{1,0:T(8,128)(2,1)S(1)}, u32[]{:S(2)}, u32[]{:S(2)}) %collective-permute-start.6) | collective-permute-done | bytes 2080 | tf_op jit(solution)/shard_map/cond/branch_0_fun/ppermute | solution.py:166
  42.8 1.3 collective-permute-done.1.sb_ref
  44.0 1.7 %collective-permute-start.10 = (bf16[256,512]{1,0:T(8,128)(2,1)}, bf16[256,512]{1,0:T(8,128)(2,1)S(1)}, u32[]{:S(2)}, u32[]{:S(2)}) collective-permute-start(bf16[256,512]{1,0:T(8,128)(2,1)} %copy-done.6), channel_id=1, source_target_pairs={{0,16},{8,24},{16,0},{24,8},{1,17},{9,25},{17,1},{25,9},{2,18},{10... | collective-permute-start | bytes 786440 | tf_op jit(solution)/shard_map/cond/branch_0_fun/ppermute | solution.py:166
  45.8 0.3 collective-permute-start.14
  46.0 7.4 %collective-permute-done.10.gc_ref = bf16[256,512]{1,0:T(8,128)(2,1)S(1)} collective-permute-done((bf16[256,512]{1,0:T(8,128)(2,1)}, bf16[256,512]{1,0:T(8,128)(2,1)S(1)}, u32[]{:S(2)}, u32[]{:S(2)}) %collective-permute-start.10) | collective-permute-done | bytes 262176 | tf_op jit(solution)/shard_map/cond/branch_0_fun/ppermute | solution.py:166
  53.4 1.7 %collective-permute-start.12 = (bf16[256,512]{1,0:T(8,128)(2,1)}, bf16[256,512]{1,0:T(8,128)(2,1)S(1)}, u32[]{:S(2)}, u32[]{:S(2)}) collective-permute-start(bf16[256,512]{1,0:T(8,128)(2,1)} %copy-done), channel_id=1, source_target_pairs={{0,16},{8,24},{16,0},{24,8},{1,17},{9,25},{17,1},{25,9},{2,18},{10... | collective-permute-start | bytes 786440 | tf_op jit(solution)/shard_map/cond/branch_0_fun/ppermute | solution.py:166
  55.1 3.9 %collective-permute-done.14.gc_ref = bf16[256,512]{1,0:T(8,128)(2,1)S(1)} collective-permute-done((bf16[256,512]{1,0:T(8,128)(2,1)}, bf16[256,512]{1,0:T(8,128)(2,1)S(1)}, u32[]{:S(2)}, u32[]{:S(2)}) %collective-permute-start.14) | collective-permute-done | bytes 262176 | tf_op jit(solution)/shard_map/cond/branch_0_fun/ppermute | solution.py:166
  59.0 2.7 %branch_0_fun.28 = (bf16[256,256]{1,0:T(8,128)(2,1)S(1)}, f32[256,256]{1,0:T(8,128)S(1)}, f32[256,256]{1,0:T(8,128)S(1)}, bf16[2048,256]{1,0:T(8,128)(2,1)S(1)}) custom-call(bf16[256,2048]{1,0:T(8,128)(2,1)} %bitcast.121, bf16[2048,512]{1,0:T(8,128)(2,1)} %bitcast.38), custom_call_target="tpu_custom_call" | custom-call | flops 536870912 | bytes 4849664 | tf_op jit(solution)/shard_map/cond/branch_0_fun/pallas_call | solution.py:175
  61.7 2.1 %collective-permute-done.12.gc_ref = bf16[256,512]{1,0:T(8,128)(2,1)S(1)} collective-permute-done((bf16[256,512]{1,0:T(8,128)(2,1)}, bf16[256,512]{1,0:T(8,128)(2,1)S(1)}, u32[]{:S(2)}, u32[]{:S(2)}) %collective-permute-start.12) | collective-permute-done | bytes 262176 | tf_op jit(solution)/shard_map/cond/branch_0_fun/ppermute | solution.py:166
  63.8 0.5 collective-permute-start.13
  64.3 0.8 branch_0_fun.34
  65.2 0.8 branch_0_fun.29
  66.0 0.3 copy-done.18
  66.3 0.3 copy-done.27
  66.7 4.1 %branch_0_fun.30 = (f32[2048,256]{1,0:T(8,128)S(1)}, f32[256,256]{1,0:T(8,128)S(1)}, f32[256,256]{1,0:T(8,128)S(1)}) custom-call(s32[1]{0:T(128)} %bitcast.me_ref, bf16[256,2048]{1,0:T(8,128)(2,1)S(1)} %bitcast.130, bf16[256,2048]{1,0:T(8,128)(2,1)} %collective-permute-done.gb_ref, bf16[256,4]{1,0:T(8,128)(2,1)S(1)} %copy.64.sa_ref, ...), custom_call_target="tpu_custom_call" | custom-call | flops 1073741824 | bytes 6033412 | tf_op jit(solution)/shard_map/cond/branch_0_fun/pallas_call | solution.py:175
  70.9 0.8 branch_0_fun.35
  71.7 0.5 collective-permute-done.7.sd_ref
  72.2 0.6 branch_0_fun.36
  72.8 0.6 branch_0_fun.37
  73.4 0.6 branch_0_fun.38
  74.0 0.6 branch_0_fun.39
  74.7 0.7 branch_0_fun.41
  75.4 0.2 collective-permute-start.16
  75.6 1.8 %branch_0_fun.31 = (f32[2048,512]{1,0:T(8,128)S(1)}, bf16[256,512]{1,0:T(8,128)(2,1)S(1)}, bf16[256,512]{1,0:T(8,128)(2,1)S(1)}) custom-call(f32[256,256]{1,0:T(8,128)S(1)} %get-tuple-element.56.ga_ref, f32[256,256]{1,0:T(8,128)S(1)} %get-tuple-element.57.gb_ref, f32[256,256]{1,0:T(8,128)S(1)} %get-tuple-element.58.fa_ref, ...), custom_call_target="tpu_custom_call" | custom-call | flops 1073741824 | bytes 8388608 | tf_op jit(solution)/shard_map/cond/branch_0_fun/pallas_call | solution.py:175
  77.5 0.7 branch_0_fun.32
  78.2 0.4 collective-permute-start.3
  78.7 1.8 %collective-permute-start.22 = (bf16[512,256]{1,0:T(8,128)(2,1)S(1)}, bf16[512,256]{1,0:T(8,128)(2,1)S(1)}, u32[]{:S(2)}, u32[]{:S(2)}) collective-permute-start(bf16[512,256]{1,0:T(8,128)(2,1)S(1)} %get-tuple-element.92.own_ref), channel_id=1, source_target_pairs={{0,1},{1,0},{2,3},{3,2},{4,5},{5,4},{6,7},{7,6},{8,9},{9,8},{10,11... | collective-permute-start | bytes 786440 | tf_op jit(solution)/shard_map/cond/branch_0_fun/ppermute | solution.py:166
  80.4 0.3 collective-permute-start.23
  80.7 0.6 branch_0_fun.47.own_ref
  81.3 1.8 %collective-permute-start.21 = (bf16[512,512]{1,0:T(8,128)(2,1)S(1)}, bf16[512,512]{1,0:T(8,128)(2,1)S(1)}, u32[]{:S(2)}, u32[]{:S(2)}) collective-permute-start(bf16[512,512]{1,0:T(8,128)(2,1)S(1)} %branch_0_fun.47.own_ref), channel_id=1, source_target_pairs={{0,1},{1,0},{2,3},{3,2},{4,5},{5,4},{6,7},{7,6},{8,9},{9,8},{10,11... | collective-permute-start | bytes 1572872 | tf_op jit(solution)/shard_map/cond/branch_0_fun/ppermute | solution.py:166
  83.1 0.8 branch_0_fun.42
  83.9 1.6 collective-permute-start.17
  85.4 2.4 %collective-permute-done.22.moved_ref = bf16[512,256]{1,0:T(8,128)(2,1)S(1)} collective-permute-done((bf16[512,256]{1,0:T(8,128)(2,1)S(1)}, bf16[512,256]{1,0:T(8,128)(2,1)S(1)}, u32[]{:S(2)}, u32[]{:S(2)}) %collective-permute-start.22) | collective-permute-done | bytes 262176 | tf_op jit(solution)/shard_map/cond/branch_0_fun/ppermute | solution.py:166
  87.8 1.8 %collective-permute-start.24 = (bf16[512,256]{1,0:T(8,128)(2,1)S(1)}, bf16[512,256]{1,0:T(8,128)(2,1)S(1)}, u32[]{:S(2)}, u32[]{:S(2)}) collective-permute-start(bf16[512,256]{1,0:T(8,128)(2,1)S(1)} %get-tuple-element.94.own_ref), channel_id=1, source_target_pairs={{0,1},{1,0},{2,3},{3,2},{4,5},{5,4},{6,7},{7,6},{8,9},{9,8},{10,11... | collective-permute-start | bytes 786440 | tf_op jit(solution)/shard_map/cond/branch_0_fun/ppermute | solution.py:166
  89.6 3.9 %collective-permute-done.23.moved_ref = bf16[512,256]{1,0:T(8,128)(2,1)S(1)} collective-permute-done((bf16[512,256]{1,0:T(8,128)(2,1)S(1)}, bf16[512,256]{1,0:T(8,128)(2,1)S(1)}, u32[]{:S(2)}, u32[]{:S(2)}) %collective-permute-start.23) | collective-permute-done | bytes 262176 | tf_op jit(solution)/shard_map/cond/branch_0_fun/ppermute | solution.py:166
  93.5 1.8 %collective-permute-start.25 = (bf16[512,256]{1,0:T(8,128)(2,1)S(1)}, bf16[512,256]{1,0:T(8,128)(2,1)S(1)}, u32[]{:S(2)}, u32[]{:S(2)}) collective-permute-start(bf16[512,256]{1,0:T(8,128)(2,1)S(1)} %get-tuple-element.95.own_ref), channel_id=1, source_target_pairs={{0,1},{1,0},{2,3},{3,2},{4,5},{5,4},{6,7},{7,6},{8,9},{9,8},{10,11... | collective-permute-start | bytes 786440 | tf_op jit(solution)/shard_map/cond/branch_0_fun/ppermute | solution.py:166
  95.2 0.6 branch_0_fun.46.own_ref
  95.8 0.6 branch_0_fun.45.own_ref
  96.4 13.9 %collective-permute-done.24.moved_ref = bf16[512,256]{1,0:T(8,128)(2,1)S(1)} collective-permute-done((bf16[512,256]{1,0:T(8,128)(2,1)S(1)}, bf16[512,256]{1,0:T(8,128)(2,1)S(1)}, u32[]{:S(2)}, u32[]{:S(2)}) %collective-permute-start.24) | collective-permute-done | bytes 262176 | tf_op jit(solution)/shard_map/cond/branch_0_fun/ppermute | solution.py:166
  110.3 1.8 %collective-permute-start.19 = (bf16[512,512]{1,0:T(8,128)(2,1)S(1)}, bf16[512,512]{1,0:T(8,128)(2,1)S(1)}, u32[]{:S(2)}, u32[]{:S(2)}) collective-permute-start(bf16[512,512]{1,0:T(8,128)(2,1)S(1)} %branch_0_fun.45.own_ref), channel_id=1, source_target_pairs={{0,1},{1,0},{2,3},{3,2},{4,5},{5,4},{6,7},{7,6},{8,9},{9,8},{10,11... | collective-permute-start | bytes 1572872 | tf_op jit(solution)/shard_map/cond/branch_0_fun/ppermute | solution.py:166
  112.1 3.9 %collective-permute-done.25.moved_ref = bf16[512,256]{1,0:T(8,128)(2,1)S(1)} collective-permute-done((bf16[512,256]{1,0:T(8,128)(2,1)S(1)}, bf16[512,256]{1,0:T(8,128)(2,1)S(1)}, u32[]{:S(2)}, u32[]{:S(2)}) %collective-permute-start.25) | collective-permute-done | bytes 262176 | tf_op jit(solution)/shard_map/cond/branch_0_fun/ppermute | solution.py:166
  115.9 1.8 %collective-permute-start.20 = (bf16[512,512]{1,0:T(8,128)(2,1)S(1)}, bf16[512,512]{1,0:T(8,128)(2,1)S(1)}, u32[]{:S(2)}, u32[]{:S(2)}) collective-permute-start(bf16[512,512]{1,0:T(8,128)(2,1)S(1)} %branch_0_fun.46.own_ref), channel_id=1, source_target_pairs={{0,1},{1,0},{2,3},{3,2},{4,5},{5,4},{6,7},{7,6},{8,9},{9,8},{10,11... | collective-permute-start | bytes 1572872 | tf_op jit(solution)/shard_map/cond/branch_0_fun/ppermute | solution.py:166
  117.7 0.6 branch_0_fun.44.own_ref
  118.3 0.3 collective-permute-start.18
  118.7 0.1 branch_0_fun.53.refs_0_
  119.0 0.2 branch_0_fun.48.refs_0_
  119.1 19.3 %collective-permute-done.20.moved_ref = bf16[512,512]{1,0:T(8,128)(2,1)S(1)} collective-permute-done((bf16[512,512]{1,0:T(8,128)(2,1)S(1)}, bf16[512,512]{1,0:T(8,128)(2,1)S(1)}, u32[]{:S(2)}, u32[]{:S(2)}) %collective-permute-start.20) | collective-permute-done | bytes 524320 | tf_op jit(solution)/shard_map/cond/branch_0_fun/ppermute | solution.py:166
  138.4 0.2 branch_0_fun.49.refs_0_
  138.6 0.2 branch_0_fun.50.refs_0_
  138.7 10.1 %collective-permute-done.18.moved_ref = bf16[512,512]{1,0:T(8,128)(2,1)S(1)} collective-permute-done((bf16[512,512]{1,0:T(8,128)(2,1)S(1)}, bf16[512,512]{1,0:T(8,128)(2,1)S(1)}, u32[]{:S(2)}, u32[]{:S(2)}) %collective-permute-start.18) | collective-permute-done | bytes 524320 | tf_op jit(solution)/shard_map/cond/branch_0_fun/ppermute | solution.py:166
  148.8 0.2 branch_0_fun.51
  149.0 1.8 %branch_0_fun.43 = bf16[256,2048]{1,0:T(8,128)(2,1)} custom-call(bf16[256,512]{1,0:T(8,128)(2,1)S(1)} %get-tuple-element.64.p_ref, bf16[2048,512]{1,0:T(8,128)(2,1)S(1)} %bitcast.49, bf16[256,2048]{1,0:T(8,128)(2,1)S(1)} %collective-permute-done.3.refs_0_, bf16[256,2048]{1,0:T(8,128)(2,1)S(1)} %collective-permute-done.17.refs_1_), custom_call_target="tpu_custom_call" | custom-call | flops 536870912 | bytes 5505024 | tf_op jit(solution)/shard_map/cond/branch_0_fun/pallas_call | solution.py:175
  (41 shorter events, 0.6 us)
Async XLA Ops:
  2.0 26.4 %collective-permute-start.8 = (bf16[256,2048]{1,0:T(8,128)(2,1)}, bf16[256,2048]{1,0:T(8,128)(2,1)S(1)}, u32[]{:S(2)}, u32[]{:S(2)}) collective-permute-start(bf16[256,2048]{1,0:T(8,128)(2,1)} %bitcast.119), channel_id=1, source_target_pairs={{0,16},{8,24},{16,0},{24,8},{1,17},{9,25},{17,1},{25,9},{2,18},{10... | collective-permute-start | bytes 3145736 | tf_op jit(solution)/shard_map/cond/branch_0_fun/ppermute | solution.py:166
  5.0 58.8 %collective-permute-start = (bf16[256,2048]{1,0:T(8,128)(2,1)}, bf16[256,2048]{1,0:T(8,128)(2,1)}, u32[]{:S(2)}, u32[]{:S(2)}) collective-permute-start(bf16[256,2048]{1,0:T(8,128)(2,1)} %bitcast.128), channel_id=1, source_target_pairs={{0,8},{8,0},{16,24},{24,16},{1,9},{9,1},{17,25},{25,17},{2,10},{10... | collective-permute-start | bytes 3145736 | tf_op jit(solution)/shard_map/cond/branch_0_fun/ppermute | solution.py:166
  5.0 60.2 %collective-permute-start.2 = (bf16[256,2048]{1,0:T(8,128)(2,1)}, bf16[256,2048]{1,0:T(8,128)(2,1)S(1)}, u32[]{:S(2)}, u32[]{:S(2)}) collective-permute-start(bf16[256,2048]{1,0:T(8,128)(2,1)} %bitcast.120), channel_id=1, source_target_pairs={{0,8},{8,0},{16,24},{24,16},{1,9},{9,1},{17,25},{25,17},{2,10},{10... | collective-permute-start | bytes 3145736 | tf_op jit(solution)/shard_map/cond/branch_0_fun/ppermute | solution.py:166
  28.4 42.5 %collective-permute-start.9 = (bf16[256,2048]{1,0:T(8,128)(2,1)S(1)}, bf16[256,2048]{1,0:T(8,128)(2,1)S(1)}, u32[]{:S(2)}, u32[]{:S(2)}) collective-permute-start(bf16[256,2048]{1,0:T(8,128)(2,1)S(1)} %collective-permute-done.8.x_ref), channel_id=1, source_target_pairs={{0,8},{8,0},{16,24},{24,16},{1,9},{9,1},{17,25},{25,17},{2,10},{10... | collective-permute-start | bytes 3145736 | tf_op jit(solution)/shard_map/cond/branch_0_fun/ppermute | solution.py:166
  30.3 0.7 copy-start
  31.0 0.7 copy-start.3
  31.7 0.7 copy-start.6
  32.4 13.3 %collective-permute-start.4 = (bf16[256,512]{1,0:T(8,128)(2,1)}, bf16[256,512]{1,0:T(8,128)(2,1)S(1)}, u32[]{:S(2)}, u32[]{:S(2)}) collective-permute-start(bf16[256,512]{1,0:T(8,128)(2,1)} %get-tuple-element.66), channel_id=1, source_target_pairs={{0,16},{8,24},{16,0},{24,8},{1,17},{9,25},{17,1},{25,9},{2,18},{10... | collective-permute-start | bytes 786440 | tf_op jit(solution)/shard_map/cond/branch_0_fun/ppermute | solution.py:166
  35.0 29.3 %copy-start.9 = (bf16[1,1,2048,512]{3,2,1,0:T(8,128)(2,1)S(1)}, bf16[1,1,2048,512]{3,2,1,0:T(8,128)(2,1)}, u32[]{:S(2)}) copy-start(bf16[1,1,2048,512]{3,2,1,0:T(8,128)(2,1)} %get-tuple-element.270) | copy-start | bytes 6291460 | tf_op jit(solution)/shard_map/cond
  35.0 7.7 %collective-permute-start.6 = (bf16[256,4]{1,0:T(8,128)(2,1)S(1)}, bf16[256,4]{1,0:T(8,128)(2,1)S(1)}, u32[]{:S(2)}, u32[]{:S(2)}) collective-permute-start(bf16[256,4]{1,0:T(8,128)(2,1)S(1)} %copy.64.sa_ref), channel_id=1, source_target_pairs={{0,16},{8,24},{16,0},{24,8},{1,17},{9,25},{17,1},{25,9},{2,18},{10... | collective-permute-start | bytes 6152 | tf_op jit(solution)/shard_map/cond/branch_0_fun/ppermute | solution.py:166
  42.8 1.3 collective-permute-start.1
  44.0 9.4 %collective-permute-start.10 = (bf16[256,512]{1,0:T(8,128)(2,1)}, bf16[256,512]{1,0:T(8,128)(2,1)S(1)}, u32[]{:S(2)}, u32[]{:S(2)}) collective-permute-start(bf16[256,512]{1,0:T(8,128)(2,1)} %copy-done.6), channel_id=1, source_target_pairs={{0,16},{8,24},{16,0},{24,8},{1,17},{9,25},{17,1},{25,9},{2,18},{10... | collective-permute-start | bytes 786440 | tf_op jit(solution)/shard_map/cond/branch_0_fun/ppermute | solution.py:166
  45.8 13.3 %collective-permute-start.14 = (bf16[256,512]{1,0:T(8,128)(2,1)}, bf16[256,512]{1,0:T(8,128)(2,1)S(1)}, u32[]{:S(2)}, u32[]{:S(2)}) collective-permute-start(bf16[256,512]{1,0:T(8,128)(2,1)} %copy-done.3), channel_id=1, source_target_pairs={{0,16},{8,24},{16,0},{24,8},{1,17},{9,25},{17,1},{25,9},{2,18},{10... | collective-permute-start | bytes 786440 | tf_op jit(solution)/shard_map/cond/branch_0_fun/ppermute | solution.py:166
  53.4 10.4 %collective-permute-start.12 = (bf16[256,512]{1,0:T(8,128)(2,1)}, bf16[256,512]{1,0:T(8,128)(2,1)S(1)}, u32[]{:S(2)}, u32[]{:S(2)}) collective-permute-start(bf16[256,512]{1,0:T(8,128)(2,1)} %copy-done), channel_id=1, source_target_pairs={{0,16},{8,24},{16,0},{24,8},{1,17},{9,25},{17,1},{25,9},{2,18},{10... | collective-permute-start | bytes 786440 | tf_op jit(solution)/shard_map/cond/branch_0_fun/ppermute | solution.py:166
  59.0 13.1 %collective-permute-start.15 = (bf16[256,512]{1,0:T(8,128)(2,1)S(1)}, bf16[256,512]{1,0:T(8,128)(2,1)S(1)}, u32[]{:S(2)}, u32[]{:S(2)}) collective-permute-start(bf16[256,512]{1,0:T(8,128)(2,1)S(1)} %collective-permute-done.14.gc_ref), channel_id=1, source_target_pairs={{0,8},{8,0},{16,24},{24,16},{1,9},{9,1},{17,25},{25,17},{2,10},{10... | collective-permute-start | bytes 786440 | tf_op jit(solution)/shard_map/cond/branch_0_fun/ppermute | solution.py:166
  63.8 9.6 %collective-permute-start.11 = (bf16[256,512]{1,0:T(8,128)(2,1)S(1)}, bf16[256,512]{1,0:T(8,128)(2,1)S(1)}, u32[]{:S(2)}, u32[]{:S(2)}) collective-permute-start(bf16[256,512]{1,0:T(8,128)(2,1)S(1)} %collective-permute-done.10.gc_ref), channel_id=1, source_target_pairs={{0,8},{8,0},{16,24},{24,16},{1,9},{9,1},{17,25},{25,17},{2,10},{10... | collective-permute-start | bytes 786440 | tf_op jit(solution)/shard_map/cond/branch_0_fun/ppermute | solution.py:166
  63.8 8.9 %collective-permute-start.13 = (bf16[256,512]{1,0:T(8,128)(2,1)S(1)}, bf16[256,512]{1,0:T(8,128)(2,1)S(1)}, u32[]{:S(2)}, u32[]{:S(2)}) collective-permute-start(bf16[256,512]{1,0:T(8,128)(2,1)S(1)} %collective-permute-done.12.gc_ref), channel_id=1, source_target_pairs={{0,8},{8,0},{16,24},{24,16},{1,9},{9,1},{17,25},{25,17},{2,10},{10... | collective-permute-start | bytes 786440 | tf_op jit(solution)/shard_map/cond/branch_0_fun/ppermute | solution.py:166
  65.1 1.2 copy-start.18
  65.1 1.5 copy-start.27
  65.2 8.8 %collective-permute-start.5 = (bf16[256,512]{1,0:T(8,128)(2,1)S(1)}, bf16[256,512]{1,0:T(8,128)(2,1)S(1)}, u32[]{:S(2)}, u32[]{:S(2)}) collective-permute-start(bf16[256,512]{1,0:T(8,128)(2,1)S(1)} %collective-permute-done.4.gc_ref), channel_id=1, source_target_pairs={{0,8},{8,0},{16,24},{24,16},{1,9},{9,1},{17,25},{25,17},{2,10},{10... | collective-permute-start | bytes 786440 | tf_op jit(solution)/shard_map/cond/branch_0_fun/ppermute | solution.py:166
  70.8 1.4 copy-start.21
  70.8 1.3 collective-permute-start.7
  75.4 7.7 %collective-permute-start.16 = (bf16[256,2048]{1,0:T(8,128)(2,1)S(1)}, bf16[256,2048]{1,0:T(8,128)(2,1)S(1)}, u32[]{:S(2)}, u32[]{:S(2)}) collective-permute-start(bf16[256,2048]{1,0:T(8,128)(2,1)S(1)} %branch_0_fun.41), channel_id=1, source_target_pairs={{0,8},{8,0},{16,24},{24,16},{1,9},{9,1},{17,25},{25,17},{2,10},{10... | collective-permute-start | bytes 3145736 | tf_op jit(solution)/shard_map/cond/branch_0_fun/ppermute | solution.py:166
  77.5 3.2 %copy-start.12 = (bf16[1,1,2048,512]{3,2,1,0:T(8,128)(2,1)S(1)}, bf16[1,1,2048,512]{3,2,1,0:T(8,128)(2,1)}, u32[]{:S(2)}) copy-start(bf16[1,1,2048,512]{3,2,1,0:T(8,128)(2,1)} %get-tuple-element.279) | copy-start | bytes 6291460 | tf_op jit(solution)/shard_map/cond
  78.2 70.8 %collective-permute-start.3 = (bf16[256,2048]{1,0:T(8,128)(2,1)S(1)}, bf16[256,2048]{1,0:T(8,128)(2,1)S(1)}, u32[]{:S(2)}, u32[]{:S(2)}) collective-permute-start(bf16[256,2048]{1,0:T(8,128)(2,1)S(1)} %branch_0_fun.32), channel_id=1, source_target_pairs={{0,8},{8,0},{16,24},{24,16},{1,9},{9,1},{17,25},{25,17},{2,10},{10... | collective-permute-start | bytes 3145736 | tf_op jit(solution)/shard_map/cond/branch_0_fun/ppermute | solution.py:166
  78.7 9.2 %collective-permute-start.22 = (bf16[512,256]{1,0:T(8,128)(2,1)S(1)}, bf16[512,256]{1,0:T(8,128)(2,1)S(1)}, u32[]{:S(2)}, u32[]{:S(2)}) collective-permute-start(bf16[512,256]{1,0:T(8,128)(2,1)S(1)} %get-tuple-element.92.own_ref), channel_id=1, source_target_pairs={{0,1},{1,0},{2,3},{3,2},{4,5},{5,4},{6,7},{7,6},{8,9},{9,8},{10,11... | collective-permute-start | bytes 786440 | tf_op jit(solution)/shard_map/cond/branch_0_fun/ppermute | solution.py:166
  80.4 13.0 %collective-permute-start.23 = (bf16[512,256]{1,0:T(8,128)(2,1)S(1)}, bf16[512,256]{1,0:T(8,128)(2,1)S(1)}, u32[]{:S(2)}, u32[]{:S(2)}) collective-permute-start(bf16[512,256]{1,0:T(8,128)(2,1)S(1)} %get-tuple-element.93.own_ref), channel_id=1, source_target_pairs={{0,1},{1,0},{2,3},{3,2},{4,5},{5,4},{6,7},{7,6},{8,9},{9,8},{10,11... | collective-permute-start | bytes 786440 | tf_op jit(solution)/shard_map/cond/branch_0_fun/ppermute | solution.py:166
  81.3 37.0 %collective-permute-start.21 = (bf16[512,512]{1,0:T(8,128)(2,1)S(1)}, bf16[512,512]{1,0:T(8,128)(2,1)S(1)}, u32[]{:S(2)}, u32[]{:S(2)}) collective-permute-start(bf16[512,512]{1,0:T(8,128)(2,1)S(1)} %branch_0_fun.47.own_ref), channel_id=1, source_target_pairs={{0,1},{1,0},{2,3},{3,2},{4,5},{5,4},{6,7},{7,6},{8,9},{9,8},{10,11... | collective-permute-start | bytes 1572872 | tf_op jit(solution)/shard_map/cond/branch_0_fun/ppermute | solution.py:166
  83.9 65.1 %collective-permute-start.17 = (bf16[256,2048]{1,0:T(8,128)(2,1)S(1)}, bf16[256,2048]{1,0:T(8,128)(2,1)S(1)}, u32[]{:S(2)}, u32[]{:S(2)}) collective-permute-start(bf16[256,2048]{1,0:T(8,128)(2,1)S(1)} %branch_0_fun.42), channel_id=1, source_target_pairs={{0,16},{8,24},{16,0},{24,8},{1,17},{9,25},{17,1},{25,9},{2,18},{10... | collective-permute-start | bytes 3145736 | tf_op jit(solution)/shard_map/cond/branch_0_fun/ppermute | solution.py:166
  87.8 22.5 %collective-permute-start.24 = (bf16[512,256]{1,0:T(8,128)(2,1)S(1)}, bf16[512,256]{1,0:T(8,128)(2,1)S(1)}, u32[]{:S(2)}, u32[]{:S(2)}) collective-permute-start(bf16[512,256]{1,0:T(8,128)(2,1)S(1)} %get-tuple-element.94.own_ref), channel_id=1, source_target_pairs={{0,1},{1,0},{2,3},{3,2},{4,5},{5,4},{6,7},{7,6},{8,9},{9,8},{10,11... | collective-permute-start | bytes 786440 | tf_op jit(solution)/shard_map/cond/branch_0_fun/ppermute | solution.py:166
  93.5 22.5 %collective-permute-start.25 = (bf16[512,256]{1,0:T(8,128)(2,1)S(1)}, bf16[512,256]{1,0:T(8,128)(2,1)S(1)}, u32[]{:S(2)}, u32[]{:S(2)}) collective-permute-start(bf16[512,256]{1,0:T(8,128)(2,1)S(1)} %get-tuple-element.95.own_ref), channel_id=1, source_target_pairs={{0,1},{1,0},{2,3},{3,2},{4,5},{5,4},{6,7},{7,6},{8,9},{9,8},{10,11... | collective-permute-start | bytes 786440 | tf_op jit(solution)/shard_map/cond/branch_0_fun/ppermute | solution.py:166
  110.3 28.3 %collective-permute-start.19 = (bf16[512,512]{1,0:T(8,128)(2,1)S(1)}, bf16[512,512]{1,0:T(8,128)(2,1)S(1)}, u32[]{:S(2)}, u32[]{:S(2)}) collective-permute-start(bf16[512,512]{1,0:T(8,128)(2,1)S(1)} %branch_0_fun.45.own_ref), channel_id=1, source_target_pairs={{0,1},{1,0},{2,3},{3,2},{4,5},{5,4},{6,7},{7,6},{8,9},{9,8},{10,11... | collective-permute-start | bytes 1572872 | tf_op jit(solution)/shard_map/cond/branch_0_fun/ppermute | solution.py:166
  115.9 22.5 %collective-permute-start.20 = (bf16[512,512]{1,0:T(8,128)(2,1)S(1)}, bf16[512,512]{1,0:T(8,128)(2,1)S(1)}, u32[]{:S(2)}, u32[]{:S(2)}) collective-permute-start(bf16[512,512]{1,0:T(8,128)(2,1)S(1)} %branch_0_fun.46.own_ref), channel_id=1, source_target_pairs={{0,1},{1,0},{2,3},{3,2},{4,5},{5,4},{6,7},{7,6},{8,9},{9,8},{10,11... | collective-permute-start | bytes 1572872 | tf_op jit(solution)/shard_map/cond/branch_0_fun/ppermute | solution.py:166
  118.3 30.6 %collective-permute-start.18 = (bf16[512,512]{1,0:T(8,128)(2,1)S(1)}, bf16[512,512]{1,0:T(8,128)(2,1)S(1)}, u32[]{:S(2)}, u32[]{:S(2)}) collective-permute-start(bf16[512,512]{1,0:T(8,128)(2,1)S(1)} %branch_0_fun.44.own_ref), channel_id=1, source_target_pairs={{0,1},{1,0},{2,3},{3,2},{4,5},{5,4},{6,7},{7,6},{8,9},{9,8},{10,11... | collective-permute-start | bytes 1572872 | tf_op jit(solution)/shard_map/cond/branch_0_fun/ppermute | solution.py:166
  118.9 19.6 %copy-start.24 = (bf16[2048,256]{1,0:T(8,128)(2,1)}, bf16[2048,256]{1,0:T(8,128)(2,1)S(1)}, u32[]{:S(2)}) copy-start(bf16[2048,256]{1,0:T(8,128)(2,1)S(1)} %branch_0_fun.55) | copy-start | bytes 3145732 | tf_op jit(solution)/shard_map/cond
  149.0 1.9 %copy-start.15 = (bf16[2048,512]{1,0:T(8,128)(2,1)}, bf16[2048,512]{1,0:T(8,128)(2,1)S(1)}, u32[]{:S(2)}) copy-start(bf16[2048,512]{1,0:T(8,128)(2,1)S(1)} %branch_0_fun.51) | copy-start | bytes 6291460 | tf_op jit(solution)/shard_map/cond
